TPU v7x, 32 devices: a whole 2x2x4 slice. The times are simulated.
32 devices in a mesh: unit: 4 (over y, core), zero: 4 (over z), cols: 2 (over x).
Axes of the slice: x: 2, y: 2, z: 4, core: 2. Of those that a mesh axis runs over, the one named last changes fastest.
Arguments:
- weight_gate: bfloat16 [20480, 13824], P(('unit', 'zero'), 'cols'), parts along dimension 0, may hold values from -0.125 to 0.125
- low_gate: bfloat16 [20480, 32], P(('unit', 'zero')), parts along dimension 0, may hold values from -0.078125 to 0.078125
- high_gate: bfloat16 [128, 13824], P('unit', 'cols'), parts along dimension 0, may hold values from -1 to 1
- weight_up: bfloat16 [20480, 13824], P(('unit', 'zero'), 'cols'), parts along dimension 0, may hold values from -0.125 to 0.125
- low_up: bfloat16 [20480, 32], P(('unit', 'zero')), parts along dimension 0, may hold values from -0.078125 to 0.078125
- high_up: bfloat16 [128, 13824], P('unit', 'cols'), parts along dimension 0, may hold values from -1 to 1
- norm_train: float32 [20480], P(('unit', 'zero', 'cols')), parts along dimension 0, may hold values from 0.25 to 1.75
- norm_step: float32 [20480], P(('unit', 'zero', 'cols')), parts along dimension 0, may hold values from -0.3 to 0.3
Outputs:
- final_gate: bfloat16 [20480, 13824], P('unit', ('cols', 'zero')), parts along dimension 0
- final_up: bfloat16 [20480, 13824], P('unit', ('cols', 'zero')), parts along dimension 0
- scale_gate: float32 [55296], P(('unit', 'cols', 'zero')), parts along dimension 0
- scale_up: float32 [55296], P(('unit', 'cols', 'zero')), parts along dimension 0
- serve_norm: bfloat16 [20480], P('unit'), parts along dimension 0
There are 4 independent parts, one for each index of `unit`. A program takes and returns all parts, laid end to end along the dimension named above; each array names one. Nothing has to cross between parts.
All inputs are finite; a program needn't handle non-finite values. Where the computation divides by a largest or mean magnitude, that divisor is 1e-20 or more.
Results may differ from a plain program's by a relative error of at most 0.001.
Values may be sent and summed in bfloat16 or wider, within the bound.
A program may use at most 192 MiB of HBM per device.

v0:
```python
import jax
import jax.numpy as jnp
from jax import lax
from jax.experimental import pallas as pl
from jax.experimental.pallas import tpu as pltpu
from jax.sharding import PartitionSpec as P

mix_rate = 0.5


def cuts(units, shares):
    total, marks, seen = sum(shares), [0], 0
    for share in shares:
        seen += share
        marks.append(units * seen // total)
    return [(a, b) for a, b in zip(marks[:-1], marks[1:]) if b > a]


def merge_kernel(block_ref, low_ref, high_ref, *refs):
    final_ref, scale_ref, result_ref = refs[-3:]
    n, _, rows = block_ref.shape
    change = mix_rate * jnp.dot(high_ref[...], low_ref[...], preferred_element_type=jnp.float32)
    total = None
    for s in range(n):
        part = block_ref[s].astype(jnp.float32) + change[:, s * rows : (s + 1) * rows]
        result_ref[:, s * rows : (s + 1) * rows] = part
        size = jnp.sum(jnp.abs(part), axis=1, keepdims=True)
        total = size if total is None else total + size
    scale = total / (n * rows)
    scale_ref[...] = scale
    final_ref[...] = (result_ref[...] / scale).astype(final_ref.dtype)


def merge(block, low, high, final, first, step, width):
    n, part, rows = block.shape
    rank = low.shape[0]
    offset = first // step
    operands = [block, low, high]
    in_specs = [
        pl.BlockSpec((n, step, rows), lambda i: (0, i, 0)),
        pl.BlockSpec((rank, n * rows), lambda i: (0, 0)),
        pl.BlockSpec((step, rank), lambda i: (i + offset, 0)),
    ]
    aliases = {}
    if final is not None:
        operands.append(final)
        in_specs.append(pl.BlockSpec(memory_space=pl.ANY))
        aliases = {3: 0}
    return pl.pallas_call(
        merge_kernel,
        grid=(part // step,),
        in_specs=in_specs,
        out_specs=[
            pl.BlockSpec((step, n * rows), lambda i: (i + offset, 0)),
            pl.BlockSpec((step, 1), lambda i: (i, 0)),
        ],
        out_shape=[
            jax.ShapeDtypeStruct((width, n * rows), jnp.bfloat16),
            jax.ShapeDtypeStruct((part, 1), jnp.float32),
        ],
        scratch_shapes=[pltpu.VMEM((step, n * rows), jnp.float32)],
        input_output_aliases=aliases,
        cost_estimate=pl.CostEstimate(
            flops=2 * part * n * rows * rank,
            bytes_accessed=4 * part * n * rows,
            transcendentals=0,
        ),
        compiler_params=pltpu.CompilerParams(vmem_limit_bytes=24 << 20),
    )(*operands)


def local(weight_gate, low_gate, high_gate, weight_up, low_up, high_up, norm_train, norm_step):
    n = lax.axis_size("zero")
    rows, width = weight_gate.shape[0], weight_gate.shape[1] // n
    rank = low_gate.shape[1]
    place = lax.axis_index("zero")
    step = next(s for s in (48, 24, 16, 8, width) if width % s == 0)

    lows = lax.all_gather(
        jnp.concatenate([low_gate.T, low_up.T], axis=0), "zero", axis=1, tiled=True
    )
    serve_norm = lax.all_gather(
        (norm_train + norm_step).astype(jnp.bfloat16), ("zero", "cols"), axis=0, tiled=True
    )
    lows, serve_norm, weight_gate, weight_up = lax.optimization_barrier(
        (lows, serve_norm, weight_gate, weight_up)
    )
    low = {"gate": lows[:rank], "up": lows[rank:]}
    high = {
        "gate": lax.dynamic_slice_in_dim(high_gate, place * width, width, axis=1).T,
        "up": lax.dynamic_slice_in_dim(high_up, place * width, width, axis=1).T,
    }
    turned = {
        "gate": weight_gate.T.reshape(n, width, rows),
        "up": weight_up.T.reshape(n, width, rows),
    }

    shares = {"gate": (1, 3), "up": (7, 2)}
    jobs = [
        (name, a * step, b * step)
        for name in ("gate", "up")
        for a, b in cuts(width // step, shares[name])
    ]
    finals = {"gate": None, "up": None}
    scales = {"gate": [], "up": []}
    block = None
    arrived = []
    for name, a, b in jobs:
        sent = turned[name][:, a:b]
        if block is not None:
            sent, block = lax.optimization_barrier((sent, block))
            arrived.append(block)
        block = lax.all_to_all(sent, "zero", split_axis=0, concat_axis=0, tiled=True)
    arrived.append(block)
    for (name, a, b), block in zip(jobs, arrived):
        finals[name], scale = merge(block, low[name], high[name], finals[name], a, step, width)
        scales[name].append(scale[:, 0])
    return (
        finals["gate"].T,
        finals["up"].T,
        jnp.concatenate(scales["gate"]),
        jnp.concatenate(scales["up"]),
        serve_norm,
    )


def solution(mesh):
    in_specs = (
        P(("unit", "zero"), "cols"),
        P(("unit", "zero"), None),
        P("unit", "cols"),
        P(("unit", "zero"), "cols"),
        P(("unit", "zero"), None),
        P("unit", "cols"),
        P(("unit", "zero", "cols")),
        P(("unit", "zero", "cols")),
    )
    out_specs = (
        P("unit", ("cols", "zero")),
        P("unit", ("cols", "zero")),
        P(("unit", "cols", "zero")),
        P(("unit", "cols", "zero")),
        P("unit"),
    )
    return jax.shard_map(local, mesh=mesh, in_specs=in_specs, out_specs=out_specs, check_vma=False)
```

profile of v0, /device:TPU:0, one launch (start us, length us, event | category | flops | bytes accessed | tf_op | source)
XLA Modules:
  0.0 875.1 jit_solution(18427595097443538595)
XLA Ops:
  0.6 0.9 pad_maximum_fusion
  1.6 19.7 %all_gather.6 = bf16[64,5120]{1,0:T(8,128)(2,1)S(1)} all-gather(bf16[64,1280]{1,0:T(8,128)(2,1)S(1)} %pad_maximum_fusion), channel_id=1, replica_groups=mesh['unit'=4,'zero'=4,'cols'=2] {'zero'}, dimensions={1}, use_global_device_ids=true | all-gather | bytes 819200 | tf_op jit(solution)/shard_map/all_gather | solution.py:79
  21.3 0.7 add_convert_fusion
  22.0 30.4 %all-gather = bf16[8,1,640]{2,1,0:T(2,128)(2,1)S(1)} all-gather(bf16[1,1,640]{2,1,0:T(2,128)(2,1)S(1)} %reshape.18), channel_id=1, replica_groups=mesh['unit'=4,'zero'=4,'cols'=2] {'zero','cols'}, dimensions={0}, use_global_device_ids=true | all-gather | bytes 11520 | tf_op jit(solution)/shard_map/all_gather | solution.py:82
  52.4 0.1 reduce
  52.5 0.6 reshape.19
  53.1 24.6 %copy.24 = bf16[6912,1280]{1,0:T(8,128)(2,1)} copy(bf16[6912,1280]{0,1:T(8,128)(2,1)} %bitcast.20) | data formatting | bytes 35389440 | tf_op jit(solution)/shard_map/transpose | solution.py:94
  77.7 4.6 slice.26
  82.4 4.9 all-to-all-start
  87.2 10.8 %slice.25 = bf16[4,1296,1280]{2,1,0:T(8,128)(2,1)} slice(bf16[4,1728,1280]{2,1,0:T(8,128)(2,1)} %bitcast.15), slice={[0:4], [432:1728], [0:1280]} | slice | bytes 26542080 | tf_op jit(solution)/shard_map/slice | solution.py:109
  98.1 78.3 %all-to-all-done.block_ref = bf16[4,432,1280]{2,1,0:T(8,128)(2,1)} async-done(((bf16[4,432,1280]{2,1,0:T(8,128)(2,1)}), bf16[4,432,1280]{2,1,0:T(8,128)(2,1)}, u32[]{:S(2)}, u32[]{:S(2)}) %all-to-all-start) | async-done | bytes 4423712 | tf_op jit(solution)/shard_map/all_to_all | solution.py:113
  176.4 6.4 all-to-all-start.1
  182.8 24.6 %copy.23 = bf16[6912,1280]{1,0:T(8,128)(2,1)} copy(bf16[6912,1280]{0,1:T(8,128)(2,1)} %bitcast.21) | data formatting | bytes 35389440 | tf_op jit(solution)/shard_map/transpose | solution.py:95
  207.4 12.5 %slice.24 = bf16[4,1344,1280]{2,1,0:T(8,128)(2,1)} slice(bf16[4,1728,1280]{2,1,0:T(8,128)(2,1)} %bitcast.16), slice={[0:4], [0:1344], [0:1280]} | slice | bytes 27525120 | tf_op jit(solution)/shard_map/slice | solution.py:109
  220.0 250.1 %all-to-all-done.1.block_ref = bf16[4,1296,1280]{2,1,0:T(8,128)(2,1)} async-done(((bf16[4,1296,1280]{2,1,0:T(8,128)(2,1)}), bf16[4,1296,1280]{2,1,0:T(8,128)(2,1)}, u32[]{:S(2)}, u32[]{:S(2)}) %all-to-all-start.1) | async-done | bytes 13271072 | tf_op jit(solution)/shard_map/all_to_all | solution.py:113
  470.1 6.5 all-to-all-start.2
  476.6 4.3 slice.27
  480.9 293.5 %all-to-all-done.2.block_ref = bf16[4,1344,1280]{2,1,0:T(8,128)(2,1)} async-done(((bf16[4,1344,1280]{2,1,0:T(8,128)(2,1)}), bf16[4,1344,1280]{2,1,0:T(8,128)(2,1)}, u32[]{:S(2)}, u32[]{:S(2)}) %all-to-all-start.2) | async-done | bytes 13762592 | tf_op jit(solution)/shard_map/all_to_all | solution.py:113
  774.4 4.8 all-to-all-start.3
  779.2 1.1 constant_dynamic-slice_fusion
  780.3 0.3 copy.28
  780.6 0.3 copy.27
  780.9 9.1 %shard_map.119 = (bf16[1728,5120]{1,0:T(8,128)(2,1)}, f32[432,1]{1,0:T(8,128)S(1)}) custom-call(bf16[4,432,1280]{2,1,0:T(8,128)(2,1)} %all-to-all-done.block_ref, bf16[32,5120]{1,0:T(8,128)(2,1)S(1)} %get-tuple-element.42.low_ref, bf16[1728,32]{1,0:T(8,128)(2,1)S(1)} %bitcast.10), custom_call_target="tpu_custom_call" | custom-call | flops 141557760 | bytes 8847360 | tf_op jit(solution)/shard_map/pallas_call | solution.py:49
  790.0 0.1 reduce.1
  790.1 24.5 %shard_map.120 = (bf16[1728,5120]{1,0:T(8,128)(2,1)}, f32[1296,1]{1,0:T(8,128)S(1)}) custom-call(bf16[4,1296,1280]{2,1,0:T(8,128)(2,1)} %all-to-all-done.1.block_ref, bf16[32,5120]{1,0:T(8,128)(2,1)S(1)} %get-tuple-element.42.low_ref, bf16[1728,32]{1,0:T(8,128)(2,1)S(1)} %bitcast.11, ...), custom_call_target="tpu_custom_call", output_to_operand_aliasing={{0}: (3, {})} | custom-call | flops 424673280 | bytes 26542080 | tf_op jit(solution)/shard_map/pallas_call | solution.py:49
  814.6 0.3 reduce.2
  814.9 0.7 pad_maximum_fusion.1
  815.6 25.0 %shard_map.121 = (bf16[1728,5120]{1,0:T(8,128)(2,1)}, f32[1344,1]{1,0:T(8,128)S(1)}) custom-call(bf16[4,1344,1280]{2,1,0:T(8,128)(2,1)} %all-to-all-done.2.block_ref, bf16[32,5120]{1,0:T(8,128)(2,1)S(1)} %get-tuple-element.41.low_ref, bf16[1728,32]{1,0:T(8,128)(2,1)S(1)} %bitcast.12), custom_call_target="tpu_custom_call" | custom-call | flops 440401920 | bytes 27525120 | tf_op jit(solution)/shard_map/pallas_call | solution.py:49
  840.6 0.3 reduce.3
  840.9 25.5 %all-to-all-done.3.block_ref = bf16[4,384,1280]{2,1,0:T(8,128)(2,1)} async-done(((bf16[4,384,1280]{2,1,0:T(8,128)(2,1)}), bf16[4,384,1280]{2,1,0:T(8,128)(2,1)}, u32[]{:S(2)}, u32[]{:S(2)}) %all-to-all-start.3) | async-done | bytes 3932192 | tf_op jit(solution)/shard_map/all_to_all | solution.py:113
  866.3 8.0 shard_map.122
  874.3 0.1 reduce.4
  874.4 0.7 pad_maximum_fusion.2
  (2 shorter events, 0.1 us)
Async XLA Ops:
  82.4 94.1 %all-to-all-start = ((bf16[4,432,1280]{2,1,0:T(8,128)(2,1)}), bf16[4,432,1280]{2,1,0:T(8,128)(2,1)}, u32[]{:S(2)}, u32[]{:S(2)}) async-start(bf16[4,432,1280]{2,1,0:T(8,128)(2,1)} %slice.26), calls=%async_computation | async-start | bytes 8847360 | tf_op jit(solution)/shard_map/all_to_all | solution.py:113
  176.4 293.7 %all-to-all-start.1 = ((bf16[4,1296,1280]{2,1,0:T(8,128)(2,1)}), bf16[4,1296,1280]{2,1,0:T(8,128)(2,1)}, u32[]{:S(2)}, u32[]{:S(2)}) async-start(bf16[4,1296,1280]{2,1,0:T(8,128)(2,1)} %slice.25), calls=%async_computation.1 | async-start | bytes 26542080 | tf_op jit(solution)/shard_map/all_to_all | solution.py:113
  470.1 304.3 %all-to-all-start.2 = ((bf16[4,1344,1280]{2,1,0:T(8,128)(2,1)}), bf16[4,1344,1280]{2,1,0:T(8,128)(2,1)}, u32[]{:S(2)}, u32[]{:S(2)}) async-start(bf16[4,1344,1280]{2,1,0:T(8,128)(2,1)} %slice.24), calls=%async_computation.2 | async-start | bytes 27525120 | tf_op jit(solution)/shard_map/all_to_all | solution.py:113
  774.4 91.9 %all-to-all-start.3 = ((bf16[4,384,1280]{2,1,0:T(8,128)(2,1)}), bf16[4,384,1280]{2,1,0:T(8,128)(2,1)}, u32[]{:S(2)}, u32[]{:S(2)}) async-start(bf16[4,384,1280]{2,1,0:T(8,128)(2,1)} %slice.27), calls=%async_computation.3 | async-start | bytes 7864320 | tf_op jit(solution)/shard_map/all_to_all | solution.py:113
where the time goes:
time: 879 us; the launch traced here: 875 us
  waiting for transfers between devices  647 us (74%)
  local copies, waits for them, and re-layouts  83.8 us (10%)
  Pallas kernels  66.6 us (8%)
  blocking collectives  50.1 us (6%)
  starting transfers between devices  22.6 us (3%)
    all_to_all x4, waiting for transfers between devices, local(): lax.all_to_all(sent, 'zero', split_axis=0, concat_axis=0, tiled=True)  647 us
    pallas_call x4, Pallas kernels, merge(): pl.pallas_call(merge_kernel, grid=(part // step,), in_specs=in_specs, out...  66.6 us
    slice x4, local copies, waits for them, and re-layouts, local(): sent = turned[name][:, a:b]  32.3 us
    all_gather x1, blocking collectives, local(): lax.all_gather((norm_train + norm_step).astype(jnp.bfloat16), ('zero', 'c...  30.4 us
    transpose x1, local copies, waits for them, and re-layouts, local(): weight_up.T.reshape(n, width, rows)  24.6 us
    transpose x1, local copies, waits for them, and re-layouts, local(): weight_gate.T.reshape(n, width, rows)  24.6 us
    all_to_all x4, starting transfers between devices, local(): lax.all_to_all(sent, 'zero', split_axis=0, concat_axis=0, tiled=True)  22.6 us
    all_gather x1, blocking collectives, local(): lax.all_gather(jnp.concatenate([low_gate.T, low_up.T], axis=0), 'zero', a...  19.7 us
  transfers between devices with their start and end apart: 4, of which 4 were waited for; matrix products, arithmetic and copies ran while one was open for 6% of the time, Pallas kernels for 7%

commit v1 on v0

--- a/solution.py
+++ b/solution.py
@@ -1,3 +1,5 @@
+import functools
+
 import jax
 import jax.numpy as jnp
 from jax import lax
@@ -69,7 +71,7 @@
     )(*operands)
 
 
-def local(weight_gate, low_gate, high_gate, weight_up, low_up, high_up, norm_train, norm_step):
+def general(weight_gate, low_gate, high_gate, weight_up, low_up, high_up, norm_train, norm_step):
     n = lax.axis_size("zero")
     rows, width = weight_gate.shape[0], weight_gate.shape[1] // n
     rank = low_gate.shape[1]
@@ -124,6 +126,394 @@
     )
 
 
+MESH = pl.DeviceIdType.MESH
+LANES, HALF, AHEAD = 128, 64, 4
+SLOTS = AHEAD + 2
+
+
+def exchange_kernel(
+    n, groups,
+    weight_gate, weight_up, low_gate, low_up, high_gate, high_up, norm_train, norm_step,
+    final, scales, norms,
+    raw, raw_pair, sent, sent_pair, lows, highs, turned, result, train, step, sums,
+    raw_sem, pair_sem, low_sem, high_sem, norm_sem,
+    send_sem, recv_sem, pair_send, pair_recv, low_send, low_recv, swap_sem, norm_send, norm_recv,
+):
+    rows, total = weight_gate.shape
+    width = total // n
+    rank = low_gate.shape[0]
+    mains = width // LANES
+    steps = 2 * mains
+    weights, own_lows, own_highs = (weight_gate, weight_up), (low_gate, low_up), (high_gate, high_up)
+    z, x = lax.axis_index("zero"), lax.axis_index("cols")
+    odd = lax.rem(z, 2)
+    here = z * groups + x
+    lanes = pl.ds(pl.multiple_of(z * rows, LANES), rows)
+
+    def peer(shift):
+        return lax.rem(z + shift, n)
+
+    def first_row(d):
+        return HALF * lax.rem(d, 2)
+
+    def pair_row(d):
+        return (width - HALF) * (1 - lax.rem(d, 2))
+
+    def load(a, s, slot, j):
+        d = peer(j)
+        tile = (d // 2) * (2 * width // LANES) + lax.rem(d, 2) * (mains + 1) + s
+        start = pl.multiple_of(tile * LANES, LANES)
+        return pltpu.make_async_copy(
+            weights[a].at[:, pl.ds(start, LANES)], raw.at[slot, j], raw_sem.at[slot, j]
+        )
+
+    def start_loads(t):
+        for a in range(2):
+            def go(a=a):
+                for j in range(n):
+                    load(a, t - a * mains, lax.rem(t, 2), j).start()
+            if isinstance(t, int):
+                if t // mains == a:
+                    go()
+            else:
+                pl.when(t // mains == a)(go)
+
+    def load_pair(a, q):
+        tile = q * (2 * width // LANES) + mains
+        return pltpu.make_async_copy(
+            weights[a].at[:, pl.ds(tile * LANES, LANES)], raw_pair.at[a, q], pair_sem.at[a, q]
+        )
+
+    def own_low(a):
+        return pltpu.make_async_copy(own_lows[a], lows.at[a, z], low_sem)
+
+    def own_high(a):
+        start = pl.multiple_of(z * width - HALF * odd, LANES)
+        return pltpu.make_async_copy(
+            own_highs[a].at[:, pl.ds(start, width + HALF)], highs.at[a], high_sem.at[a]
+        )
+
+    def bulk(t, j):
+        d = peer(j)
+        a = t // mains
+        row = pl.multiple_of(first_row(d) + LANES * (t - a * mains), HALF)
+        slot = lax.rem(t, SLOTS)
+        return pltpu.make_async_remote_copy(
+            src_ref=sent.at[slot, j - 1],
+            dst_ref=final.at[a, pl.ds(row, LANES), lanes],
+            send_sem=send_sem.at[slot, j - 1],
+            recv_sem=recv_sem.at[t, j - 1],
+            device_id={"zero": d},
+            device_id_type=MESH,
+        )
+
+    def pair(a, j):
+        d = peer(j)
+        return pltpu.make_async_remote_copy(
+            src_ref=sent_pair.at[a, d // 2, pl.ds(pl.multiple_of(first_row(d), HALF), HALF)],
+            dst_ref=final.at[a, pl.ds(pl.multiple_of(pair_row(d), HALF), HALF), lanes],
+            send_sem=pair_send.at[a, j - 1],
+            recv_sem=pair_recv.at[a, j - 1],
+            device_id={"zero": d},
+            device_id_type=MESH,
+        )
+
+    def low_copy(block, d, index):
+        return pltpu.make_async_remote_copy(
+            src_ref=lows.at[x, block],
+            dst_ref=lows.at[x, block],
+            send_sem=low_send.at[index],
+            recv_sem=low_recv.at[block],
+            device_id={"zero": d},
+            device_id_type=MESH,
+        )
+
+    def low_swap():
+        return pltpu.make_async_remote_copy(
+            src_ref=lows.at[x],
+            dst_ref=lows.at[x],
+            send_sem=swap_sem.at[0],
+            recv_sem=swap_sem.at[1],
+            device_id={"cols": 1 - x},
+            device_id_type=MESH,
+        )
+
+    def norm_copy(i):
+        there = lax.rem(here + i, n * groups)
+        return pltpu.make_async_remote_copy(
+            src_ref=sums.at[here],
+            dst_ref=sums.at[here],
+            send_sem=norm_send.at[i - 1],
+            recv_sem=norm_recv.at[i - 1],
+            device_id={"zero": there // groups, "cols": lax.rem(there, groups)},
+            device_id_type=MESH,
+        )
+
+    def prepare(t, reused):
+        slot, from_slot, a = lax.rem(t, SLOTS), lax.rem(t, 2), t // mains
+        row = pl.multiple_of(first_row(z) + LANES * (t - a * mains), HALF)
+        if reused:
+            for j in range(1, n):
+                bulk(t - SLOTS, j).wait_send()
+        for j in range(n):
+            load(0, 0, from_slot, j).wait()
+            part = raw[from_slot, j].T
+            if j:
+                sent[slot, j - 1] = part
+            else:
+                final[a, pl.ds(row, LANES), lanes] = part
+
+    def prepare_pair(a):
+        for q in range(n // 2):
+            load_pair(a, q).wait()
+            sent_pair[a, q] = raw_pair[a, q].T
+        own = sent_pair[a, z // 2, pl.ds(pl.multiple_of(first_row(z), HALF), HALF), :]
+        final[a, pl.ds(pl.multiple_of(pair_row(z), HALF), HALF), lanes] = own
+
+    def merge(a, row):
+        row = pl.multiple_of(row, HALF)
+        high = turned[a, pl.ds(pl.multiple_of(row + HALF * odd, HALF), HALF), :]
+        size = None
+        for s in range(n):
+            cut = slice(s * rows, (s + 1) * rows)
+            change = mix_rate * jnp.dot(high, lows[a, s], preferred_element_type=jnp.float32)
+            part = final[a, pl.ds(row, HALF), cut].astype(jnp.float32) + change
+            result[:, cut] = part
+            here_size = jnp.sum(jnp.abs(part), axis=1, keepdims=True)
+            size = here_size if size is None else size + here_size
+        scale = size / (n * rows)
+        scales[a, pl.ds(row, HALF), :] = scale
+        inverse = 1.0 / scale
+        for s in range(n):
+            cut = slice(s * rows, (s + 1) * rows)
+            final[a, pl.ds(row, HALF), cut] = (result[:, cut] * inverse).astype(final.dtype)
+
+    def finish(t):
+        for j in range(1, n):
+            bulk(t, j).wait_recv()
+        a = t // mains
+        row = first_row(z) + LANES * (t - a * mains)
+        lax.fori_loop(0, LANES // HALF, lambda i, c: (merge(a, row + HALF * i), c)[1], 0)
+
+    def finish_pair(a):
+        for j in range(1, n):
+            pair(a, j).wait_recv()
+        merge(a, pair_row(z))
+
+    def send(t):
+        for j in reversed(range(1, n)):
+            bulk(t, j).start()
+
+    def send_pair(a):
+        for j in reversed(range(1, n)):
+            pair(a, j).start()
+
+    barrier = pltpu.get_barrier_semaphore()
+    for i in range(1, n * groups):
+        there = lax.rem(here + i, n * groups)
+        pl.semaphore_signal(
+            barrier, inc=1,
+            device_id={"zero": there // groups, "cols": lax.rem(there, groups)},
+            device_id_type=MESH,
+        )
+    for q in range(n // 2):
+        load_pair(0, q).start()
+    for a in range(2):
+        pl.when(x == a)(lambda a=a: own_low(a).start())
+    start_loads(0)
+    start_loads(1)
+    norm_loads = [
+        pltpu.make_async_copy(norm_train, train, norm_sem.at[0]),
+        pltpu.make_async_copy(norm_step, step, norm_sem.at[1]),
+    ]
+    for copy in norm_loads:
+        copy.start()
+    for a in range(2):
+        own_high(a).start()
+    for q in range(n // 2):
+        load_pair(1, q).start()
+
+    prepare_pair(0)
+    for copy in norm_loads:
+        copy.wait()
+    sums[here] = train[...] + step[...]
+    own_low(0).wait()
+    pl.semaphore_wait(barrier, n * groups - 1)
+
+    mate, inner = z + 1 - 2 * odd, (z == 1) | (z == 2)
+    gateway, other = 2 - z // 2, 2 - 2 * (z // 2)
+    low_copy(z, gateway, 0).start()
+    low_copy(z, mate, 1).start()
+    send_pair(0)
+    prepare(0, False)
+    start_loads(2)
+    for i in range(1, n * groups):
+        norm_copy(i).start()
+    prepare(1, False)
+    start_loads(3)
+    send(0)
+
+    @pl.when(inner)
+    def _():
+        for i in range(2):
+            low_copy(other + i, mate, 2 + i).wait_recv()
+            low_copy(other + i, mate, 2 + i).start()
+
+    prepare(2, False)
+    start_loads(4)
+    send(1)
+    for a in range(2):
+        own_high(a).wait()
+        turned[a] = highs[a].T
+    prepare(3, False)
+    start_loads(5)
+    send(2)
+    prepare_pair(1)
+
+    low_copy(mate, mate, 0).wait_recv()
+
+    @pl.when(jnp.logical_not(inner))
+    def _():
+        for i in range(2):
+            low_copy(other + i, mate, 2 + i).wait_recv()
+
+    low_swap().start()
+    prepare(4, False)
+    start_loads(6)
+    send(3)
+    low_swap().wait_recv()
+    finish_pair(0)
+
+    def at(k, carry):
+        send(k + AHEAD)
+        prepare(k + AHEAD + 1, True)
+
+        @pl.when(k + AHEAD + 3 < steps)
+        def _():
+            start_loads(k + AHEAD + 3)
+
+        finish(k)
+        return carry
+
+    send(4)
+    prepare(5, False)
+    start_loads(7)
+    finish(0)
+    lax.fori_loop(1, steps - AHEAD - 1, at, 0)
+    send(steps - 1)
+    send_pair(1)
+    lax.fori_loop(steps - AHEAD - 1, steps, lambda k, c: (finish(k), c)[1], 0)
+
+    for i in range(1, n * groups):
+        norm_copy(i).wait_recv()
+    for i in range(n * groups):
+        length = sums.shape[2]
+        norms[:, i * length : (i + 1) * length] = sums[i].astype(norms.dtype)
+    finish_pair(1)
+
+    for t in range(steps - SLOTS, steps):
+        for j in range(1, n):
+            bulk(t, j).wait_send()
+    for a in range(2):
+        for j in range(1, n):
+            pair(a, j).wait_send()
+    low_copy(z, gateway, 0).wait_send()
+    low_copy(z, mate, 1).wait_send()
+
+    @pl.when(inner)
+    def _():
+        for i in range(2):
+            low_copy(other + i, mate, 2 + i).wait_send()
+
+    low_swap().wait_send()
+    for i in range(1, n * groups):
+        norm_copy(i).wait_send()
+
+
+def place_kernel(final, gate, up, sem):
+    copies = [
+        pltpu.make_async_copy(final.at[a], out, sem.at[a]) for a, out in enumerate((gate, up))
+    ]
+    for copy in copies:
+        copy.start()
+    for copy in copies:
+        copy.wait()
+
+
+def exchange(weight_gate, low_gate, high_gate, weight_up, low_up, high_up, norm_train, norm_step):
+    n, groups = lax.axis_size("zero"), lax.axis_size("cols")
+    rows, width = weight_gate.shape[0], weight_gate.shape[1] // n
+    rank, length = low_gate.shape[1], norm_train.shape[0]
+    steps = 2 * (width // LANES)
+    dma = pltpu.SemaphoreType.DMA
+    bf16, f32 = jnp.bfloat16, jnp.float32
+    final, scales, norms = pl.pallas_call(
+        functools.partial(exchange_kernel, n, groups),
+        in_specs=[pl.BlockSpec(memory_space=pl.ANY)] * 8,
+        out_specs=[pl.BlockSpec(memory_space=pltpu.VMEM)] * 3,
+        out_shape=[
+            pltpu.VMEM((2, width, n * rows), bf16),
+            pltpu.VMEM((2, width, 1), f32),
+            pltpu.VMEM((1, n * groups * length), bf16),
+        ],
+        scratch_shapes=[
+            pltpu.VMEM((2, n, rows, LANES), bf16),
+            pltpu.VMEM((2, n // 2, rows, LANES), bf16),
+            pltpu.VMEM((SLOTS, n - 1, LANES, rows), bf16),
+            pltpu.VMEM((2, n // 2, LANES, rows), bf16),
+            pltpu.VMEM((2, n, rank, rows), bf16),
+            pltpu.VMEM((2, rank, width + HALF), bf16),
+            pltpu.VMEM((2, width + HALF, rank), bf16),
+            pltpu.VMEM((HALF, n * rows), f32),
+            pltpu.VMEM((1, length), f32),
+            pltpu.VMEM((1, length), f32),
+            pltpu.VMEM((n * groups, 1, length), f32),
+            dma((2, n)),
+            dma((2, n // 2)),
+            dma,
+            dma((2,)),
+            dma((2,)),
+            dma((SLOTS, n - 1)),
+            dma((steps, n - 1)),
+            dma((2, n - 1)),
+            dma((2, n - 1)),
+            dma((4,)),
+            dma((n,)),
+            dma((2,)),
+            dma((n * groups - 1,)),
+            dma((n * groups - 1,)),
+        ],
+        cost_estimate=pl.CostEstimate(
+            flops=4 * width * n * rows * rank,
+            bytes_accessed=8 * width * n * rows,
+            transcendentals=0,
+        ),
+        compiler_params=pltpu.CompilerParams(
+            collective_id=0, has_side_effects=True, vmem_limit_bytes=26 << 20
+        ),
+    )(
+        weight_gate, weight_up, low_gate.T, low_up.T, high_gate, high_up,
+        norm_train.reshape(1, length), norm_step.reshape(1, length),
+    )
+    gate, up = pl.pallas_call(
+        place_kernel,
+        in_specs=[pl.BlockSpec(memory_space=pltpu.VMEM)],
+        out_specs=[pl.BlockSpec(memory_space=pl.ANY)] * 2,
+        out_shape=[jax.ShapeDtypeStruct((width, n * rows), bf16)] * 2,
+        scratch_shapes=[dma((2,))],
+        compiler_params=pltpu.CompilerParams(vmem_limit_bytes=2 << 20),
+    )(final)
+    return gate.T, up.T, scales[0, :, 0], scales[1, :, 0], norms.reshape(-1)
+
+
+def local(*args):
+    n, groups = lax.axis_size("zero"), lax.axis_size("cols")
+    rows, total = args[0].shape
+    if n == 4 and groups == 2 and rows % LANES == 0 and (total // n) % LANES == HALF:
+        return exchange(*args)
+    return general(*args)
+
+
 def solution(mesh):
     in_specs = (
         P(("unit", "zero"), "cols"),

time: 879 us -> 790 us (0.90)
  Pallas kernels: 66.6 us -> 785 us
  waiting for transfers between devices: 647 us -> 0 us
  local copies, waits for them, and re-layouts: 83.8 us -> 3.68 us
  blocking collectives: 50.1 us -> 0 us
  starting transfers between devices: 22.6 us -> 0 us
    pallas_call x4 -> x2, Pallas kernels: 66.6 us -> 785 us  [the longest x1 772 us: exchange(): pl.pallas_call(functools.partial(exchange_kernel, n, groups), in_specs=[p...]
    all_to_all x4 -> x0, waiting for transfers between devices: 647 us -> none  [local(): lax.all_to_all(sent, 'zero', split_axis=0, concat_axis=0, tiled=True)]
    all_gather x2 -> x0, blocking collectives: 50.1 us -> none  [the longest x1 30.4 us: local(): lax.all_gather((norm_train + norm_step).astype(jnp.bfloat16), ('zero', 'c...]
    transpose x2 -> x0, local copies, waits for them, and re-layouts: 49.2 us -> none  [the longest x1 24.6 us: local(): weight_up.T.reshape(n, width, rows)]
    slice x5 -> x1, local copies, waits for them, and re-layouts: 32.3 us -> 1.15 us  [exchange(): return (gate.T, up.T, scales[0, :, 0], scales[1, :, 0], norms.reshape(-1))]
    all_to_all x4 -> x0, starting transfers between devices: 22.6 us -> none  [local(): lax.all_to_all(sent, 'zero', split_axis=0, concat_axis=0, tiled=True)]
  transfers between devices with their start and end apart: 4 -> 0, of which waited for: 4 -> 0; matrix products, arithmetic and copies ran while one was open for 6% -> 0% of each run, Pallas kernels for 7% -> 0%
where the time goes in v1:
time: 790 us
  Pallas kernels  785 us (99%)
    pallas_call x1, Pallas kernels, exchange(): pl.pallas_call(functools.partial(exchange_kernel, n, groups), in_specs=[p...  772 us

profile of v1, /device:TPU:0, one launch (start us, length us, event | category | flops | bytes accessed | tf_op | source)
XLA Modules:
  0.0 789.5 jit_solution(13960326144180709516)
XLA Ops:
  0.6 1.3 reshape.19.norm_train
  1.9 1.3 reshape.20.norm_step
  3.2 772.2 %shard_map.119 = (bf16[2,1728,5120]{2,1,0:T(8,128)(2,1)S(1)}, f32[2,1728,1]{2,1,0:T(8,128)S(1)}, bf16[1,5120]{1,0:T(2,128)(2,1)S(1)}) custom-call(bf16[1280,6912]{1,0:T(8,128)(2,1)} %weight_gate.1, bf16[1280,6912]{1,0:T(8,128)(2,1)} %weight_up.1, bf16[32,1280]{1,0:T(8,128)(2,1)} %bitcast.4, bf16[32,1280]{1,0:T(8,128)(2,1)} %bitcast.5, ...), custom_call_target="tpu_custom_call" | custom-call | flops 1132462080 | bytes 70778880 | tf_op jit(solution)/shard_map/pallas_call | solution.py:450
  775.4 12.3 %shard_map.120 = (bf16[1728,5120]{1,0:T(8,128)(2,1)}, bf16[1728,5120]{1,0:T(8,128)(2,1)}) custom-call(bf16[2,1728,5120]{2,1,0:T(8,128)(2,1)S(1)} %get-tuple-element.10.final), custom_call_target="tpu_custom_call" | custom-call | tf_op jit(solution)/shard_map/pallas_call | solution.py:498
  787.7 0.7 reduce.2
  788.4 1.1 slice_reduce_fusion

commit v2 on v1

--- a/solution.py
+++ b/solution.py
@@ -127,21 +127,39 @@
 
 
 MESH = pl.DeviceIdType.MESH
-LANES, HALF, AHEAD = 128, 64, 4
+LANES, HALF, LAST, AHEAD, PIECES = 128, 64, 32, 4, 4
 SLOTS = AHEAD + 2
+
+
+def peer(z, n, shift):
+    return lax.rem(z + shift, n)
+
+
+def first_row(d):
+    return HALF * lax.rem(d, 2)
+
+
+def pair_row(d, width):
+    return pl.multiple_of((width - HALF) * (1 - lax.rem(d, 2)), HALF)
+
+
+def enter(places):
+    barrier = pltpu.get_barrier_semaphore()
+    for place in places:
+        pl.semaphore_signal(barrier, inc=1, device_id=place, device_id_type=MESH)
+    return lambda: pl.semaphore_wait(barrier, len(places))
 
 
 def exchange_kernel(
     n, groups,
     weight_gate, weight_up, low_gate, low_up, high_gate, high_up, norm_train, norm_step,
-    final, scales, norms,
-    raw, raw_pair, sent, sent_pair, lows, highs, turned, result, train, step, sums,
+    final, scales, sums,
+    raw, raw_pair, sent, sent_pair, lows, highs, turned, result, train, step,
     raw_sem, pair_sem, low_sem, high_sem, norm_sem,
     send_sem, recv_sem, pair_send, pair_recv, low_send, low_recv, swap_sem, norm_send, norm_recv,
 ):
     rows, total = weight_gate.shape
     width = total // n
-    rank = low_gate.shape[0]
     mains = width // LANES
     steps = 2 * mains
     weights, own_lows, own_highs = (weight_gate, weight_up), (low_gate, low_up), (high_gate, high_up)
@@ -150,17 +168,12 @@
     here = z * groups + x
     lanes = pl.ds(pl.multiple_of(z * rows, LANES), rows)
 
-    def peer(shift):
-        return lax.rem(z + shift, n)
-
-    def first_row(d):
-        return HALF * lax.rem(d, 2)
-
-    def pair_row(d):
-        return (width - HALF) * (1 - lax.rem(d, 2))
+    def place(i):
+        there = lax.rem(here + i, n * groups)
+        return {"zero": there // groups, "cols": lax.rem(there, groups)}
 
     def load(a, s, slot, j):
-        d = peer(j)
+        d = peer(z, n, j)
         tile = (d // 2) * (2 * width // LANES) + lax.rem(d, 2) * (mains + 1) + s
         start = pl.multiple_of(tile * LANES, LANES)
         return pltpu.make_async_copy(
@@ -168,15 +181,15 @@
         )
 
     def start_loads(t):
-        for a in range(2):
-            def go(a=a):
-                for j in range(n):
-                    load(a, t - a * mains, lax.rem(t, 2), j).start()
-            if isinstance(t, int):
-                if t // mains == a:
-                    go()
-            else:
-                pl.when(t // mains == a)(go)
+        def go(a):
+            for j in reversed(range(n)):
+                load(a, t - a * mains, lax.rem(t, 2), j).start()
+
+        if isinstance(t, int):
+            go(t // mains)
+        else:
+            for a in range(2):
+                pl.when(t // mains == a)(functools.partial(go, a))
 
     def load_pair(a, q):
         tile = q * (2 * width // LANES) + mains
@@ -194,7 +207,7 @@
         )
 
     def bulk(t, j):
-        d = peer(j)
+        d = peer(z, n, j)
         a = t // mains
         row = pl.multiple_of(first_row(d) + LANES * (t - a * mains), HALF)
         slot = lax.rem(t, SLOTS)
@@ -207,13 +220,16 @@
             device_id_type=MESH,
         )
 
-    def pair(a, j):
-        d = peer(j)
+    def pair(a, j, cut=0, height=HALF):
+        d = peer(z, n, j)
+        source = pl.multiple_of(first_row(d) + cut, height)
+        target = pl.multiple_of(pair_row(d, width) + cut, height)
+        index = a + cut // height
         return pltpu.make_async_remote_copy(
-            src_ref=sent_pair.at[a, d // 2, pl.ds(pl.multiple_of(first_row(d), HALF), HALF)],
-            dst_ref=final.at[a, pl.ds(pl.multiple_of(pair_row(d), HALF), HALF), lanes],
-            send_sem=pair_send.at[a, j - 1],
-            recv_sem=pair_recv.at[a, j - 1],
+            src_ref=sent_pair.at[a, d // 2, pl.ds(source, height)],
+            dst_ref=final.at[a, pl.ds(target, height), lanes],
+            send_sem=pair_send.at[index, j - 1],
+            recv_sem=pair_recv.at[index, j - 1],
             device_id={"zero": d},
             device_id_type=MESH,
         )
@@ -239,87 +255,73 @@
         )
 
     def norm_copy(i):
-        there = lax.rem(here + i, n * groups)
         return pltpu.make_async_remote_copy(
             src_ref=sums.at[here],
             dst_ref=sums.at[here],
             send_sem=norm_send.at[i - 1],
             recv_sem=norm_recv.at[i - 1],
-            device_id={"zero": there // groups, "cols": lax.rem(there, groups)},
+            device_id=place(i),
             device_id_type=MESH,
         )
 
     def prepare(t, reused):
         slot, from_slot, a = lax.rem(t, SLOTS), lax.rem(t, 2), t // mains
-        row = pl.multiple_of(first_row(z) + LANES * (t - a * mains), HALF)
         if reused:
             for j in range(1, n):
                 bulk(t - SLOTS, j).wait_send()
-        for j in range(n):
+        for j in reversed(range(n)):
             load(0, 0, from_slot, j).wait()
             part = raw[from_slot, j].T
             if j:
                 sent[slot, j - 1] = part
             else:
+                row = pl.multiple_of(first_row(z) + LANES * (t - a * mains), HALF)
                 final[a, pl.ds(row, LANES), lanes] = part
 
     def prepare_pair(a):
         for q in range(n // 2):
             load_pair(a, q).wait()
             sent_pair[a, q] = raw_pair[a, q].T
+
+    def keep_pair(a):
         own = sent_pair[a, z // 2, pl.ds(pl.multiple_of(first_row(z), HALF), HALF), :]
-        final[a, pl.ds(pl.multiple_of(pair_row(z), HALF), HALF), lanes] = own
-
-    def merge(a, row):
-        row = pl.multiple_of(row, HALF)
-        high = turned[a, pl.ds(pl.multiple_of(row + HALF * odd, HALF), HALF), :]
+        final[a, pl.ds(pair_row(z, width), HALF), lanes] = own
+
+    def merge(a, row, height):
+        row = pl.multiple_of(row, height)
+        span = pl.ds(row, height)
+        high = turned[a, pl.ds(pl.multiple_of(row + HALF * odd, height), height), :]
         size = None
         for s in range(n):
             cut = slice(s * rows, (s + 1) * rows)
             change = mix_rate * jnp.dot(high, lows[a, s], preferred_element_type=jnp.float32)
-            part = final[a, pl.ds(row, HALF), cut].astype(jnp.float32) + change
-            result[:, cut] = part
-            here_size = jnp.sum(jnp.abs(part), axis=1, keepdims=True)
-            size = here_size if size is None else size + here_size
+            part = final[a, span, cut].astype(jnp.float32) + change
+            result[:height, cut] = part
+            mine = jnp.sum(jnp.abs(part), axis=1, keepdims=True)
+            size = mine if size is None else size + mine
         scale = size / (n * rows)
-        scales[a, pl.ds(row, HALF), :] = scale
+        scales[a, span, :] = scale
         inverse = 1.0 / scale
         for s in range(n):
             cut = slice(s * rows, (s + 1) * rows)
-            final[a, pl.ds(row, HALF), cut] = (result[:, cut] * inverse).astype(final.dtype)
+            final[a, span, cut] = (result[:height, cut] * inverse).astype(final.dtype)
 
     def finish(t):
         for j in range(1, n):
             bulk(t, j).wait_recv()
         a = t // mains
         row = first_row(z) + LANES * (t - a * mains)
-        lax.fori_loop(0, LANES // HALF, lambda i, c: (merge(a, row + HALF * i), c)[1], 0)
-
-    def finish_pair(a):
-        for j in range(1, n):
-            pair(a, j).wait_recv()
-        merge(a, pair_row(z))
+        lax.fori_loop(0, LANES // HALF, lambda i, c: (merge(a, row + HALF * i, HALF), c)[1], 0)
 
     def send(t):
         for j in reversed(range(1, n)):
             bulk(t, j).start()
 
-    def send_pair(a):
-        for j in reversed(range(1, n)):
-            pair(a, j).start()
-
-    barrier = pltpu.get_barrier_semaphore()
-    for i in range(1, n * groups):
-        there = lax.rem(here + i, n * groups)
-        pl.semaphore_signal(
-            barrier, inc=1,
-            device_id={"zero": there // groups, "cols": lax.rem(there, groups)},
-            device_id_type=MESH,
-        )
+    wait_for_all = enter([place(i) for i in range(1, n * groups)])
+    for a in range(2):
+        pl.when(x == a)(lambda a=a: own_low(a).start())
     for q in range(n // 2):
         load_pair(0, q).start()
-    for a in range(2):
-        pl.when(x == a)(lambda a=a: own_low(a).start())
     start_loads(0)
     start_loads(1)
     norm_loads = [
@@ -333,18 +335,19 @@
     for q in range(n // 2):
         load_pair(1, q).start()
 
+    mate, inner = z + 1 - 2 * odd, (z == 1) | (z == 2)
+    gateway, other = 2 - z // 2, 2 - 2 * (z // 2)
+    own_low(0).wait()
     prepare_pair(0)
+    wait_for_all()
+    low_copy(z, gateway, 0).start()
+    low_copy(z, mate, 1).start()
     for copy in norm_loads:
         copy.wait()
-    sums[here] = train[...] + step[...]
-    own_low(0).wait()
-    pl.semaphore_wait(barrier, n * groups - 1)
-
-    mate, inner = z + 1 - 2 * odd, (z == 1) | (z == 2)
-    gateway, other = 2 - z // 2, 2 - 2 * (z // 2)
-    low_copy(z, gateway, 0).start()
-    low_copy(z, mate, 1).start()
-    send_pair(0)
+    sums[here] = (train[...] + step[...]).reshape(1, -1)
+    for j in reversed(range(1, n)):
+        pair(0, j).start()
+    keep_pair(0)
     prepare(0, False)
     start_loads(2)
     for i in range(1, n * groups):
@@ -359,16 +362,17 @@
             low_copy(other + i, mate, 2 + i).wait_recv()
             low_copy(other + i, mate, 2 + i).start()
 
-    prepare(2, False)
-    start_loads(4)
-    send(1)
+    t = 2
+    while t < AHEAD + 1:
+        prepare(t, False)
+        start_loads(t + 2)
+        send(t - 1)
+        t += 1
     for a in range(2):
         own_high(a).wait()
         turned[a] = highs[a].T
-    prepare(3, False)
-    start_loads(5)
-    send(2)
     prepare_pair(1)
+    keep_pair(1)
 
     low_copy(mate, mate, 0).wait_recv()
 
@@ -378,11 +382,15 @@
             low_copy(other + i, mate, 2 + i).wait_recv()
 
     low_swap().start()
-    prepare(4, False)
-    start_loads(6)
-    send(3)
     low_swap().wait_recv()
-    finish_pair(0)
+    for j in range(1, n):
+        pair(0, j).wait_recv()
+    merge(0, pair_row(z, width), HALF)
+
+    send(AHEAD)
+    prepare(AHEAD + 1, False)
+    start_loads(AHEAD + 3)
+    finish(0)
 
     def at(k, carry):
         send(k + AHEAD)
@@ -395,28 +403,20 @@
         finish(k)
         return carry
 
-    send(4)
-    prepare(5, False)
-    start_loads(7)
-    finish(0)
     lax.fori_loop(1, steps - AHEAD - 1, at, 0)
     send(steps - 1)
-    send_pair(1)
-    lax.fori_loop(steps - AHEAD - 1, steps, lambda k, c: (finish(k), c)[1], 0)
-
+    for part in range(2):
+        for j in reversed(range(1, n)):
+            pair(1, j, part * LAST, LAST).start()
     for i in range(1, n * groups):
         norm_copy(i).wait_recv()
-    for i in range(n * groups):
-        length = sums.shape[2]
-        norms[:, i * length : (i + 1) * length] = sums[i].astype(norms.dtype)
-    finish_pair(1)
+    lax.fori_loop(steps - AHEAD - 1, steps, lambda k, c: (finish(k), c)[1], 0)
 
     for t in range(steps - SLOTS, steps):
         for j in range(1, n):
             bulk(t, j).wait_send()
-    for a in range(2):
-        for j in range(1, n):
-            pair(a, j).wait_send()
+    for j in range(1, n):
+        pair(0, j).wait_send()
     low_copy(z, gateway, 0).wait_send()
     low_copy(z, mate, 1).wait_send()
 
@@ -428,14 +428,42 @@
     low_swap().wait_send()
     for i in range(1, n * groups):
         norm_copy(i).wait_send()
-
-
-def place_kernel(final, gate, up, sem):
+    for part in range(2):
+        for j in range(1, n):
+            pair(1, j, part * LAST, LAST).wait_recv()
+        merge(1, pair_row(z, width) + part * LAST, LAST)
+    for part in range(2):
+        for j in range(1, n):
+            pair(1, j, part * LAST, LAST).wait_send()
+
+
+def to_lanes(column):
+    n = column.shape[0]
+    if n < LANES:
+        column = jnp.concatenate([column, jnp.zeros((LANES - n, 1), column.dtype)], axis=0)
+    return jnp.broadcast_to(column, (LANES, LANES)).T[0, :n]
+
+
+def place_kernel(final, scales, sums, gate, up, scale_gate, scale_up, norm, sem):
+    width = scale_gate.shape[0]
     copies = [
-        pltpu.make_async_copy(final.at[a], out, sem.at[a]) for a, out in enumerate((gate, up))
+        pltpu.make_async_copy(
+            final.at[a, pl.ds(i * width // PIECES, width // PIECES)],
+            out.at[pl.ds(i * width // PIECES, width // PIECES)],
+            sem.at[a, i],
+        )
+        for i in range(PIECES)
+        for a, out in enumerate((gate, up))
     ]
     for copy in copies:
         copy.start()
+    for a, out in enumerate((scale_gate, scale_up)):
+        for k in range(0, width, LANES):
+            w = min(LANES, width - k)
+            out[pl.ds(k, w)] = to_lanes(scales[a, pl.ds(k, w), :])
+    length = sums.shape[2]
+    for i in range(sums.shape[0]):
+        norm[pl.ds(i * length, length)] = sums[i, 0].astype(norm.dtype)
     for copy in copies:
         copy.wait()
 
@@ -447,14 +475,15 @@
     steps = 2 * (width // LANES)
     dma = pltpu.SemaphoreType.DMA
     bf16, f32 = jnp.bfloat16, jnp.float32
-    final, scales, norms = pl.pallas_call(
+    vmem, hbm = pl.BlockSpec(memory_space=pltpu.VMEM), pl.BlockSpec(memory_space=pl.ANY)
+    final, scales, sums = pl.pallas_call(
         functools.partial(exchange_kernel, n, groups),
-        in_specs=[pl.BlockSpec(memory_space=pl.ANY)] * 8,
-        out_specs=[pl.BlockSpec(memory_space=pltpu.VMEM)] * 3,
+        in_specs=[hbm] * 8,
+        out_specs=[vmem] * 3,
         out_shape=[
             pltpu.VMEM((2, width, n * rows), bf16),
             pltpu.VMEM((2, width, 1), f32),
-            pltpu.VMEM((1, n * groups * length), bf16),
+            pltpu.VMEM((n * groups, 1, length), f32),
         ],
         scratch_shapes=[
             pltpu.VMEM((2, n, rows, LANES), bf16),
@@ -465,9 +494,8 @@
             pltpu.VMEM((2, rank, width + HALF), bf16),
             pltpu.VMEM((2, width + HALF, rank), bf16),
             pltpu.VMEM((HALF, n * rows), f32),
-            pltpu.VMEM((1, length), f32),
-            pltpu.VMEM((1, length), f32),
-            pltpu.VMEM((n * groups, 1, length), f32),
+            pltpu.VMEM((length,), f32),
+            pltpu.VMEM((length,), f32),
             dma((2, n)),
             dma((2, n // 2)),
             dma,
@@ -475,8 +503,8 @@
             dma((2,)),
             dma((SLOTS, n - 1)),
             dma((steps, n - 1)),
-            dma((2, n - 1)),
-            dma((2, n - 1)),
+            dma((3, n - 1)),
+            dma((3, n - 1)),
             dma((4,)),
             dma((n,)),
             dma((2,)),
@@ -489,21 +517,24 @@
             transcendentals=0,
         ),
         compiler_params=pltpu.CompilerParams(
-            collective_id=0, has_side_effects=True, vmem_limit_bytes=26 << 20
+            collective_id=0, has_side_effects=True, vmem_limit_bytes=24 << 20
         ),
-    )(
-        weight_gate, weight_up, low_gate.T, low_up.T, high_gate, high_up,
-        norm_train.reshape(1, length), norm_step.reshape(1, length),
-    )
-    gate, up = pl.pallas_call(
+    )(weight_gate, weight_up, low_gate.T, low_up.T, high_gate, high_up, norm_train, norm_step)
+    gate, up, scale_gate, scale_up, norm = pl.pallas_call(
         place_kernel,
-        in_specs=[pl.BlockSpec(memory_space=pltpu.VMEM)],
-        out_specs=[pl.BlockSpec(memory_space=pl.ANY)] * 2,
-        out_shape=[jax.ShapeDtypeStruct((width, n * rows), bf16)] * 2,
-        scratch_shapes=[dma((2,))],
-        compiler_params=pltpu.CompilerParams(vmem_limit_bytes=2 << 20),
-    )(final)
-    return gate.T, up.T, scales[0, :, 0], scales[1, :, 0], norms.reshape(-1)
+        in_specs=[vmem] * 3,
+        out_specs=[hbm] * 2 + [vmem] * 3,
+        out_shape=[
+            jax.ShapeDtypeStruct((width, n * rows), bf16),
+            jax.ShapeDtypeStruct((width, n * rows), bf16),
+            jax.ShapeDtypeStruct((width,), f32),
+            jax.ShapeDtypeStruct((width,), f32),
+            jax.ShapeDtypeStruct((n * groups * length,), bf16),
+        ],
+        scratch_shapes=[dma((2, PIECES))],
+        compiler_params=pltpu.CompilerParams(vmem_limit_bytes=24 << 20),
+    )(*(pltpu.with_memory_space_constraint(v, pltpu.VMEM) for v in (final, scales, sums)))
+    return gate.T, up.T, scale_gate, scale_up, norm
 
 
 def local(*args):

time: 790 us -> 785 us (level)
  no operation moved by 1% of the time
where the time goes in v2:
time: 785 us
  Pallas kernels  784 us (100%)
    pallas_call x1, Pallas kernels, exchange(): pl.pallas_call(functools.partial(exchange_kernel, n, groups), in_specs=[h...  772 us

profile of v2, /device:TPU:0, one launch (start us, length us, event | category | flops | bytes accessed | tf_op | source)
XLA Modules:
  0.0 785.1 jit_solution(15331091867344556393)
XLA Ops:
  0.6 772.2 %shard_map.119 = (bf16[2,1728,5120]{2,1,0:T(8,128)(2,1)S(1)}, f32[2,1728,1]{2,1,0:T(8,128)S(1)}, f32[8,1,640]{2,1,0:T(1,128)S(1)}) custom-call(bf16[1280,6912]{1,0:T(8,128)(2,1)} %weight_gate.1, bf16[1280,6912]{1,0:T(8,128)(2,1)} %weight_up.1, bf16[32,1280]{1,0:T(8,128)(2,1)} %bitcast.4, bf16[32,1280]{1,0:T(8,128)(2,1)} %bitcast.5, ...), custom_call_target="tpu_custom_call" | custom-call | flops 1132462080 | bytes 70778880 | tf_op jit(solution)/shard_map/pallas_call | solution.py:479
  772.9 12.2 %shard_map.120 = (bf16[1728,5120]{1,0:T(8,128)(2,1)}, bf16[1728,5120]{1,0:T(8,128)(2,1)}, f32[1728]{0:T(1024)}, f32[1728]{0:T(1024)}, bf16[5120]{0:T(1024)(128)(2,1)}) custom-call(bf16[2,1728,5120]{2,1,0:T(8,128)(2,1)S(1)} %get-tuple-element.13.final, f32[2,1728,1]{2,1,0:T(8,128)S(1)} %get-tuple-element.14.scales, f32[8,1,640]{2,1,0:T(1,128)S(1)} %get-tuple-element.15.sums), custom_call_target="tpu_custom_call" | custom-call | tf_op jit(solution)/shard_map/pallas_call | solution.py:523

commit v3 on v2

--- a/solution.py
+++ b/solution.py
@@ -127,7 +127,7 @@
 
 
 MESH = pl.DeviceIdType.MESH
-LANES, HALF, LAST, AHEAD, PIECES = 128, 64, 32, 4, 4
+LANES, HALF, AHEAD, PIECES, GRANT = 128, 64, 4, 4, 22 << 20
 SLOTS = AHEAD + 2
 
 
@@ -150,13 +150,33 @@
     return lambda: pl.semaphore_wait(barrier, len(places))
 
 
+def combine(source, row, high, lows, result, target, place):
+    n, _, rows = lows.shape
+    span = pl.ds(row, HALF)
+    size = None
+    for s in range(n):
+        cut = slice(s * rows, (s + 1) * rows)
+        change = mix_rate * jnp.dot(high, lows[s], preferred_element_type=jnp.float32)
+        part = source[span, cut].astype(jnp.float32) + change
+        result[:, cut] = part
+        mine = jnp.sum(jnp.abs(part), axis=1, keepdims=True)
+        size = mine if size is None else size + mine
+    scale = size / (n * rows)
+    inverse = 1.0 / scale
+    for s in range(n):
+        cut = slice(s * rows, (s + 1) * rows)
+        target[pl.ds(place, HALF), cut] = (result[:, cut] * inverse).astype(target.dtype)
+    return scale
+
+
 def exchange_kernel(
     n, groups,
     weight_gate, weight_up, low_gate, low_up, high_gate, high_up, norm_train, norm_step,
-    final, scales, sums,
-    raw, raw_pair, sent, sent_pair, lows, highs, turned, result, train, step,
+    final, scales, sums, lows, turned, piece_0, piece_1, piece_2, piece_3,
+    raw, raw_pair, sent, sent_pair, highs, result, train, step,
     raw_sem, pair_sem, low_sem, high_sem, norm_sem,
     send_sem, recv_sem, pair_send, pair_recv, low_send, low_recv, swap_sem, norm_send, norm_recv,
+    piece_sem,
 ):
     rows, total = weight_gate.shape
     width = total // n
@@ -220,19 +240,23 @@
             device_id_type=MESH,
         )
 
-    def pair(a, j, cut=0, height=HALF):
+    def pair_of(a, d):
+        return sent_pair.at[a, d // 2, pl.ds(pl.multiple_of(first_row(d), HALF), HALF)]
+
+    def pair(j):
         d = peer(z, n, j)
-        source = pl.multiple_of(first_row(d) + cut, height)
-        target = pl.multiple_of(pair_row(d, width) + cut, height)
-        index = a + cut // height
         return pltpu.make_async_remote_copy(
-            src_ref=sent_pair.at[a, d // 2, pl.ds(source, height)],
-            dst_ref=final.at[a, pl.ds(target, height), lanes],
-            send_sem=pair_send.at[index, j - 1],
-            recv_sem=pair_recv.at[index, j - 1],
+            src_ref=pair_of(0, d),
+            dst_ref=final.at[0, pl.ds(pair_row(d, width), HALF), lanes],
+            send_sem=pair_send.at[j - 1],
+            recv_sem=pair_recv.at[j - 1],
             device_id={"zero": d},
             device_id_type=MESH,
         )
+
+    def piece_copy(j):
+        out = (piece_0, piece_1, piece_2, piece_3)[j]
+        return pltpu.make_async_copy(pair_of(1, peer(z, n, j)), out, piece_sem.at[j])
 
     def low_copy(block, d, index):
         return pltpu.make_async_remote_copy(
@@ -287,31 +311,18 @@
         own = sent_pair[a, z // 2, pl.ds(pl.multiple_of(first_row(z), HALF), HALF), :]
         final[a, pl.ds(pair_row(z, width), HALF), lanes] = own
 
-    def merge(a, row, height):
-        row = pl.multiple_of(row, height)
-        span = pl.ds(row, height)
-        high = turned[a, pl.ds(pl.multiple_of(row + HALF * odd, height), height), :]
-        size = None
-        for s in range(n):
-            cut = slice(s * rows, (s + 1) * rows)
-            change = mix_rate * jnp.dot(high, lows[a, s], preferred_element_type=jnp.float32)
-            part = final[a, span, cut].astype(jnp.float32) + change
-            result[:height, cut] = part
-            mine = jnp.sum(jnp.abs(part), axis=1, keepdims=True)
-            size = mine if size is None else size + mine
-        scale = size / (n * rows)
-        scales[a, span, :] = scale
-        inverse = 1.0 / scale
-        for s in range(n):
-            cut = slice(s * rows, (s + 1) * rows)
-            final[a, span, cut] = (result[:height, cut] * inverse).astype(final.dtype)
+    def merge_at(a, row):
+        row = pl.multiple_of(row, HALF)
+        high = turned[a, pl.ds(pl.multiple_of(row + HALF * odd, HALF), HALF), :]
+        scale = combine(final.at[a], row, high, lows.at[a], result, final.at[a], row)
+        scales[a, pl.ds(row, HALF), :] = scale
 
     def finish(t):
         for j in range(1, n):
             bulk(t, j).wait_recv()
         a = t // mains
         row = first_row(z) + LANES * (t - a * mains)
-        lax.fori_loop(0, LANES // HALF, lambda i, c: (merge(a, row + HALF * i, HALF), c)[1], 0)
+        lax.fori_loop(0, LANES // HALF, lambda i, c: (merge_at(a, row + HALF * i), c)[1], 0)
 
     def send(t):
         for j in reversed(range(1, n)):
@@ -346,7 +357,7 @@
         copy.wait()
     sums[here] = (train[...] + step[...]).reshape(1, -1)
     for j in reversed(range(1, n)):
-        pair(0, j).start()
+        pair(j).start()
     keep_pair(0)
     prepare(0, False)
     start_loads(2)
@@ -372,7 +383,6 @@
         own_high(a).wait()
         turned[a] = highs[a].T
     prepare_pair(1)
-    keep_pair(1)
 
     low_copy(mate, mate, 0).wait_recv()
 
@@ -383,9 +393,11 @@
 
     low_swap().start()
     low_swap().wait_recv()
+    for j in range(n):
+        piece_copy(j).start()
     for j in range(1, n):
-        pair(0, j).wait_recv()
-    merge(0, pair_row(z, width), HALF)
+        pair(j).wait_recv()
+    merge_at(0, pair_row(z, width))
 
     send(AHEAD)
     prepare(AHEAD + 1, False)
@@ -405,18 +417,19 @@
 
     lax.fori_loop(1, steps - AHEAD - 1, at, 0)
     send(steps - 1)
-    for part in range(2):
-        for j in reversed(range(1, n)):
-            pair(1, j, part * LAST, LAST).start()
+    for j in range(n):
+        piece_copy(j).wait()
     for i in range(1, n * groups):
         norm_copy(i).wait_recv()
-    lax.fori_loop(steps - AHEAD - 1, steps, lambda k, c: (finish(k), c)[1], 0)
+    lax.fori_loop(steps - AHEAD - 1, steps - 1, lambda k, c: (finish(k), c)[1], 0)
+    for j in range(1, n):
+        bulk(steps - 1, j).wait_recv()
 
     for t in range(steps - SLOTS, steps):
         for j in range(1, n):
             bulk(t, j).wait_send()
     for j in range(1, n):
-        pair(0, j).wait_send()
+        pair(j).wait_send()
     low_copy(z, gateway, 0).wait_send()
     low_copy(z, mate, 1).wait_send()
 
@@ -428,13 +441,6 @@
     low_swap().wait_send()
     for i in range(1, n * groups):
         norm_copy(i).wait_send()
-    for part in range(2):
-        for j in range(1, n):
-            pair(1, j, part * LAST, LAST).wait_recv()
-        merge(1, pair_row(z, width) + part * LAST, LAST)
-    for part in range(2):
-        for j in range(1, n):
-            pair(1, j, part * LAST, LAST).wait_send()
 
 
 def to_lanes(column):
@@ -444,28 +450,74 @@
     return jnp.broadcast_to(column, (LANES, LANES)).T[0, :n]
 
 
-def place_kernel(final, scales, sums, gate, up, scale_gate, scale_up, norm, sem):
+def place_kernel(
+    final, scales, sums, lows, turned,
+    gate, up, scale_gate, norm, late_scale,
+    late, result, sem, late_sem,
+):
     width = scale_gate.shape[0]
+    odd = lax.rem(lax.axis_index("zero"), 2)
+    early = width // LANES * LANES - LANES
     copies = [
         pltpu.make_async_copy(
-            final.at[a, pl.ds(i * width // PIECES, width // PIECES)],
-            out.at[pl.ds(i * width // PIECES, width // PIECES)],
+            final.at[a, pl.ds(i * height // PIECES, height // PIECES)],
+            out.at[pl.ds(i * height // PIECES, height // PIECES)],
             sem.at[a, i],
         )
         for i in range(PIECES)
-        for a, out in enumerate((gate, up))
+        for a, (out, height) in enumerate(((gate, width), (up, early)))
     ]
+    between = pltpu.make_async_copy(
+        final.at[1, pl.ds(early, HALF)], up.at[pl.ds(early, HALF)], late_sem.at[0]
+    )
+    row = pl.multiple_of(early + HALF * odd, HALF)
+    rest = pltpu.make_async_copy(late, up.at[pl.ds(row, LANES)], late_sem.at[1])
     for copy in copies:
         copy.start()
-    for a, out in enumerate((scale_gate, scale_up)):
-        for k in range(0, width, LANES):
-            w = min(LANES, width - k)
-            out[pl.ds(k, w)] = to_lanes(scales[a, pl.ds(k, w), :])
+    pl.when(odd == 1)(lambda: between.start())
+    for i in range(LANES // HALF):
+        start = pl.multiple_of(row + HALF * i, HALF)
+        high = turned[1, pl.ds(pl.multiple_of(start + HALF * odd, HALF), HALF), :]
+        scale = combine(final.at[1], start, high, lows.at[1], result, late, HALF * i)
+        late_scale[pl.ds(HALF * i, HALF), :] = scale
+    for k in range(0, width, LANES):
+        w = min(LANES, width - k)
+        scale_gate[pl.ds(k, w)] = to_lanes(scales[0, pl.ds(k, w), :])
     length = sums.shape[2]
     for i in range(sums.shape[0]):
         norm[pl.ds(i * length, length)] = sums[i, 0].astype(norm.dtype)
+    rest.start()
     for copy in copies:
         copy.wait()
+    pl.when(odd == 1)(lambda: between.wait())
+    rest.wait()
+
+
+def last_kernel(
+    n, up_in, own, from_1, from_2, from_3, lows, turned, scales, late_scale,
+    up, scale_up, final, result, sem,
+):
+    del up_in
+    rows, width = own.shape[1], scale_up.shape[0]
+    z = lax.axis_index("zero")
+    row = pair_row(z, width)
+    for j, piece in enumerate((own, from_1, from_2, from_3)):
+        start = pl.multiple_of(peer(z, n, n - j) * rows, LANES)
+        final[:, pl.ds(start, rows)] = piece[...]
+    high = turned[1, pl.ds(pl.multiple_of(row + first_row(z), HALF), HALF), :]
+    scale = combine(final, 0, high, lows.at[1], result, final, 0)
+    copy = pltpu.make_async_copy(final, up.at[pl.ds(row, HALF)], sem)
+    copy.start()
+    for k in range(0, width, LANES):
+        w = min(LANES, width - k)
+        scale_up[pl.ds(k, w)] = to_lanes(scales[1, pl.ds(k, w), :])
+    late = to_lanes(late_scale[...])
+    for odd, place in ((0, width - HALF), (1, 0)):
+        @pl.when(lax.rem(z, 2) == odd)
+        def _(odd=odd, place=place):
+            scale_up[pl.ds(width - LANES - HALF * (1 - odd), LANES)] = late
+            scale_up[pl.ds(place, HALF)] = to_lanes(scale)
+    copy.wait()
 
 
 def exchange(weight_gate, low_gate, high_gate, weight_up, low_up, high_up, norm_train, norm_step):
@@ -476,23 +528,29 @@
     dma = pltpu.SemaphoreType.DMA
     bf16, f32 = jnp.bfloat16, jnp.float32
     vmem, hbm = pl.BlockSpec(memory_space=pltpu.VMEM), pl.BlockSpec(memory_space=pl.ANY)
-    final, scales, sums = pl.pallas_call(
+    work = pl.CostEstimate(
+        flops=4 * width * n * rows * rank,
+        bytes_accessed=8 * width * n * rows,
+        transcendentals=0,
+    )
+    final, scales, sums, lows, turned, own, *pieces = pl.pallas_call(
         functools.partial(exchange_kernel, n, groups),
         in_specs=[hbm] * 8,
-        out_specs=[vmem] * 3,
+        out_specs=[vmem] * 5 + [hbm] * n,
         out_shape=[
             pltpu.VMEM((2, width, n * rows), bf16),
             pltpu.VMEM((2, width, 1), f32),
             pltpu.VMEM((n * groups, 1, length), f32),
-        ],
+            pltpu.VMEM((2, n, rank, rows), bf16),
+            pltpu.VMEM((2, width + HALF, rank), bf16),
+        ]
+        + [jax.ShapeDtypeStruct((HALF, rows), bf16)] * n,
         scratch_shapes=[
             pltpu.VMEM((2, n, rows, LANES), bf16),
             pltpu.VMEM((2, n // 2, rows, LANES), bf16),
             pltpu.VMEM((SLOTS, n - 1, LANES, rows), bf16),
             pltpu.VMEM((2, n // 2, LANES, rows), bf16),
-            pltpu.VMEM((2, n, rank, rows), bf16),
             pltpu.VMEM((2, rank, width + HALF), bf16),
-            pltpu.VMEM((2, width + HALF, rank), bf16),
             pltpu.VMEM((HALF, n * rows), f32),
             pltpu.VMEM((length,), f32),
             pltpu.VMEM((length,), f32),
@@ -503,37 +561,64 @@
             dma((2,)),
             dma((SLOTS, n - 1)),
             dma((steps, n - 1)),
-            dma((3, n - 1)),
-            dma((3, n - 1)),
+            dma((n - 1,)),
+            dma((n - 1,)),
             dma((4,)),
             dma((n,)),
             dma((2,)),
             dma((n * groups - 1,)),
             dma((n * groups - 1,)),
+            dma((n,)),
         ],
-        cost_estimate=pl.CostEstimate(
-            flops=4 * width * n * rows * rank,
-            bytes_accessed=8 * width * n * rows,
-            transcendentals=0,
-        ),
+        cost_estimate=work,
         compiler_params=pltpu.CompilerParams(
-            collective_id=0, has_side_effects=True, vmem_limit_bytes=24 << 20
+            collective_id=0, has_side_effects=True, vmem_limit_bytes=GRANT
         ),
     )(weight_gate, weight_up, low_gate.T, low_up.T, high_gate, high_up, norm_train, norm_step)
-    gate, up, scale_gate, scale_up, norm = pl.pallas_call(
+    arrived = [
+        lax.ppermute(pieces[j - 1], "zero", [(i, (i + j) % n) for i in range(n)])
+        for j in reversed(range(1, n))
+    ][::-1]
+    final, scales, sums, lows, turned = (
+        pltpu.with_memory_space_constraint(v, pltpu.VMEM)
+        for v in (final, scales, sums, lows, turned)
+    )
+    gate, up, scale_gate, norm, late_scale = pl.pallas_call(
         place_kernel,
-        in_specs=[vmem] * 3,
+        in_specs=[vmem] * 5,
         out_specs=[hbm] * 2 + [vmem] * 3,
         out_shape=[
             jax.ShapeDtypeStruct((width, n * rows), bf16),
             jax.ShapeDtypeStruct((width, n * rows), bf16),
             jax.ShapeDtypeStruct((width,), f32),
+            jax.ShapeDtypeStruct((n * groups * length,), bf16),
+            pltpu.VMEM((LANES, 1), f32),
+        ],
+        scratch_shapes=[
+            pltpu.VMEM((LANES, n * rows), bf16),
+            pltpu.VMEM((HALF, n * rows), f32),
+            dma((2, PIECES)),
+            dma((2,)),
+        ],
+        cost_estimate=work,
+        compiler_params=pltpu.CompilerParams(vmem_limit_bytes=GRANT),
+    )(final, scales, sums, lows, turned)
+    up, scale_up = pl.pallas_call(
+        functools.partial(last_kernel, n),
+        in_specs=[hbm] + [vmem] * 8,
+        out_specs=[hbm, vmem],
+        out_shape=[
+            jax.ShapeDtypeStruct((width, n * rows), bf16),
             jax.ShapeDtypeStruct((width,), f32),
-            jax.ShapeDtypeStruct((n * groups * length,), bf16),
         ],
-        scratch_shapes=[dma((2, PIECES))],
-        compiler_params=pltpu.CompilerParams(vmem_limit_bytes=24 << 20),
-    )(*(pltpu.with_memory_space_constraint(v, pltpu.VMEM) for v in (final, scales, sums)))
+        scratch_shapes=[
+            pltpu.VMEM((HALF, n * rows), bf16),
+            pltpu.VMEM((HALF, n * rows), f32),
+            dma,
+        ],
+        input_output_aliases={0: 0},
+        compiler_params=pltpu.CompilerParams(vmem_limit_bytes=GRANT),
+    )(up, own, *arrived, lows, turned, scales, late_scale)
     return gate.T, up.T, scale_gate, scale_up, norm
 
 

time: 785 us -> 777 us (0.990)
  Pallas kernels: 784 us -> 772 us
    pallas_call x1, Pallas kernels: 772 us -> 758 us  [exchange(): pl.pallas_call(functools.partial(exchange_kernel, n, groups), in_specs=[h...]
  transfers between devices with their start and end apart: 0 -> 3, of which waited for: 0 -> 0; matrix products, arithmetic and copies ran while one was open for 0% -> 0% of each run, Pallas kernels for 0% -> 2%
where the time goes in v3:
time: 777 us
  Pallas kernels  772 us (99%)
    pallas_call x1, Pallas kernels, exchange(): pl.pallas_call(functools.partial(exchange_kernel, n, groups), in_specs=[h...  758 us
  transfers between devices with their start and end apart: 3, of which 0 were waited for; matrix products, arithmetic and copies ran while one was open for 0% of the time, Pallas kernels for 2%

profile of v3, /device:TPU:0, one launch (start us, length us, event | category | flops | bytes accessed | tf_op | source)
XLA Modules:
  0.0 776.9 jit_solution(12175132070504841692)
XLA Ops:
  0.6 757.8 %shard_map.119 = (bf16[2,1728,5120]{2,1,0:T(8,128)(2,1)S(1)}, f32[2,1728,1]{2,1,0:T(8,128)S(1)}, f32[8,1,640]{2,1,0:T(1,128)S(1)}, bf16[2,4,32,1280]{3,2,1,0:T(8...) custom-call(bf16[1280,6912]{1,0:T(8,128)(2,1)} %weight_gate.1, ...), custom_call_target="tpu_custom_call" | custom-call | flops 1132462080 | bytes 70778880 | tf_op jit(solution)/shard_map/pallas_call | solution.py:536
  758.4 0.1 collective-permute-start
  758.5 1.4 collective-permute-start.1
  759.9 2.8 collective-permute-start.2
  762.8 0.0 copy-start
  762.8 12.0 %shard_map.120 = (bf16[1728,5120]{1,0:T(8,128)(2,1)}, bf16[1728,5120]{1,0:T(8,128)(2,1)}, f32[1728]{0:T(1024)}, bf16[5120]{0:T(1024)(128)(2,1)}, f32[128,1]{1,0:T(8,128)S(1)}) custom-call(bf16[2,1728,5120]{2,1,0:T(8,128)(2,1)S(1)} %get-tuple-element.21.final, f32[2,1728,1]{2,1,0:T(8,128)S(1)} %get-tuple-element.22.scales, ...), custom_call_target="tpu_custom_call" | custom-call | flops 1132462080 | bytes 70778880 | tf_op jit(solution)/shard_map/pallas_call | solution.py:586
  774.8 0.0 collective-permute-done.from_1
  774.8 0.0 collective-permute-done.1.from_2
  774.8 0.0 collective-permute-done.2.from_3
  774.8 0.0 copy-done
  774.8 2.1 shard_map.121
Async XLA Ops:
  758.4 16.3 %collective-permute-start = (bf16[64,1280]{1,0:T(8,128)(2,1)}, bf16[64,1280]{1,0:T(8,128)(2,1)S(1)}, u32[]{:S(2)}, u32[]{:S(2)}) collective-permute-start(bf16[64,1280]{1,0:T(8,128)(2,1)} %get-tuple-element.29), channel_id=1, source_target_pairs={{0,2},{2,4},{4,6},{6,0},{1,3},{3,5},{5,7},{7,1},{8,10},{10,12},{12... | collective-permute-start | bytes 491528 | tf_op jit(solution)/shard_map/ppermute | solution.py:579
  758.5 16.3 %collective-permute-start.1 = (bf16[64,1280]{1,0:T(8,128)(2,1)}, bf16[64,1280]{1,0:T(8,128)(2,1)S(1)}, u32[]{:S(2)}, u32[]{:S(2)}) collective-permute-start(bf16[64,1280]{1,0:T(8,128)(2,1)} %get-tuple-element.30), channel_id=1, source_target_pairs={{0,4},{2,6},{4,0},{6,2},{1,5},{3,7},{5,1},{7,3},{8,12},{10,14},{12... | collective-permute-start | bytes 491528 | tf_op jit(solution)/shard_map/ppermute | solution.py:579
  759.9 14.9 %collective-permute-start.2 = (bf16[64,1280]{1,0:T(8,128)(2,1)}, bf16[64,1280]{1,0:T(8,128)(2,1)S(1)}, u32[]{:S(2)}, u32[]{:S(2)}) collective-permute-start(bf16[64,1280]{1,0:T(8,128)(2,1)} %get-tuple-element.31), channel_id=1, source_target_pairs={{0,6},{2,0},{4,2},{6,4},{1,7},{3,1},{5,3},{7,5},{8,14},{10,8},{12,... | collective-permute-start | bytes 491528 | tf_op jit(solution)/shard_map/ppermute | solution.py:579
  762.8 12.0 %copy-start = (bf16[64,1280]{1,0:T(8,128)(2,1)S(1)}, bf16[64,1280]{1,0:T(8,128)(2,1)}, u32[]{:S(2)}) copy-start(bf16[64,1280]{1,0:T(8,128)(2,1)} %get-tuple-element.28.own) | copy-start | bytes 491524

commit v4 on v3

--- a/solution.py
+++ b/solution.py
@@ -172,11 +172,11 @@
 def exchange_kernel(
     n, groups,
     weight_gate, weight_up, low_gate, low_up, high_gate, high_up, norm_train, norm_step,
-    final, scales, sums, lows, turned, piece_0, piece_1, piece_2, piece_3,
+    final, scales, sums, lows, turned, near, own_piece, piece_2, piece_3,
     raw, raw_pair, sent, sent_pair, highs, result, train, step,
     raw_sem, pair_sem, low_sem, high_sem, norm_sem,
     send_sem, recv_sem, pair_send, pair_recv, low_send, low_recv, swap_sem, norm_send, norm_recv,
-    piece_sem,
+    piece_sem, near_sem,
 ):
     rows, total = weight_gate.shape
     width = total // n
@@ -254,9 +254,19 @@
             device_id_type=MESH,
         )
 
-    def piece_copy(j):
-        out = (piece_0, piece_1, piece_2, piece_3)[j]
-        return pltpu.make_async_copy(pair_of(1, peer(z, n, j)), out, piece_sem.at[j])
+    def piece_copy(i):
+        d, out = ((z, own_piece), (peer(z, n, n // 2), piece_2), (n - 1 - z, piece_3))[i]
+        return pltpu.make_async_copy(pair_of(1, d), out, piece_sem.at[i])
+
+    def near_copy():
+        return pltpu.make_async_remote_copy(
+            src_ref=pair_of(1, mate),
+            dst_ref=near,
+            send_sem=near_sem.at[0],
+            recv_sem=near_sem.at[1],
+            device_id={"zero": mate},
+            device_id_type=MESH,
+        )
 
     def low_copy(block, d, index):
         return pltpu.make_async_remote_copy(
@@ -393,8 +403,9 @@
 
     low_swap().start()
     low_swap().wait_recv()
-    for j in range(n):
-        piece_copy(j).start()
+    near_copy().start()
+    for i in range(3):
+        piece_copy(i).start()
     for j in range(1, n):
         pair(j).wait_recv()
     merge_at(0, pair_row(z, width))
@@ -417,8 +428,9 @@
 
     lax.fori_loop(1, steps - AHEAD - 1, at, 0)
     send(steps - 1)
-    for j in range(n):
-        piece_copy(j).wait()
+    for i in range(3):
+        piece_copy(i).wait()
+    near_copy().wait()
     for i in range(1, n * groups):
         norm_copy(i).wait_recv()
     lax.fori_loop(steps - AHEAD - 1, steps - 1, lambda k, c: (finish(k), c)[1], 0)
@@ -494,15 +506,17 @@
 
 
 def last_kernel(
-    n, up_in, own, from_1, from_2, from_3, lows, turned, scales, late_scale,
+    n, up_in, near, own, from_2, from_3, lows, turned, scales, late_scale,
     up, scale_up, final, result, sem,
 ):
     del up_in
     rows, width = own.shape[1], scale_up.shape[0]
     z = lax.axis_index("zero")
     row = pair_row(z, width)
-    for j, piece in enumerate((own, from_1, from_2, from_3)):
-        start = pl.multiple_of(peer(z, n, n - j) * rows, LANES)
+    mate = z + 1 - 2 * lax.rem(z, 2)
+    sources = ((z, own), (mate, near), (peer(z, n, n // 2), from_2), (n - 1 - z, from_3))
+    for source, piece in sources:
+        start = pl.multiple_of(source * rows, LANES)
         final[:, pl.ds(start, rows)] = piece[...]
     high = turned[1, pl.ds(pl.multiple_of(row + first_row(z), HALF), HALF), :]
     scale = combine(final, 0, high, lows.at[1], result, final, 0)
@@ -533,18 +547,19 @@
         bytes_accessed=8 * width * n * rows,
         transcendentals=0,
     )
-    final, scales, sums, lows, turned, own, *pieces = pl.pallas_call(
+    final, scales, sums, lows, turned, near, own, *pieces = pl.pallas_call(
         functools.partial(exchange_kernel, n, groups),
         in_specs=[hbm] * 8,
-        out_specs=[vmem] * 5 + [hbm] * n,
+        out_specs=[vmem] * 6 + [hbm] * 3,
         out_shape=[
             pltpu.VMEM((2, width, n * rows), bf16),
             pltpu.VMEM((2, width, 1), f32),
             pltpu.VMEM((n * groups, 1, length), f32),
             pltpu.VMEM((2, n, rank, rows), bf16),
             pltpu.VMEM((2, width + HALF, rank), bf16),
+            pltpu.VMEM((HALF, rows), bf16),
         ]
-        + [jax.ShapeDtypeStruct((HALF, rows), bf16)] * n,
+        + [jax.ShapeDtypeStruct((HALF, rows), bf16)] * 3,
         scratch_shapes=[
             pltpu.VMEM((2, n, rows, LANES), bf16),
             pltpu.VMEM((2, n // 2, rows, LANES), bf16),
@@ -568,7 +583,8 @@
             dma((2,)),
             dma((n * groups - 1,)),
             dma((n * groups - 1,)),
-            dma((n,)),
+            dma((3,)),
+            dma((2,)),
         ],
         cost_estimate=work,
         compiler_params=pltpu.CompilerParams(
@@ -576,12 +592,12 @@
         ),
     )(weight_gate, weight_up, low_gate.T, low_up.T, high_gate, high_up, norm_train, norm_step)
     arrived = [
-        lax.ppermute(pieces[j - 1], "zero", [(i, (i + j) % n) for i in range(n)])
-        for j in reversed(range(1, n))
-    ][::-1]
-    final, scales, sums, lows, turned = (
+        lax.ppermute(pieces[0], "zero", [(i, (i + n // 2) % n) for i in range(n)]),
+        lax.ppermute(pieces[1], "zero", [(i, n - 1 - i) for i in range(n)]),
+    ]
+    final, scales, sums, lows, turned, near = (
         pltpu.with_memory_space_constraint(v, pltpu.VMEM)
-        for v in (final, scales, sums, lows, turned)
+        for v in (final, scales, sums, lows, turned, near)
     )
     gate, up, scale_gate, norm, late_scale = pl.pallas_call(
         place_kernel,
@@ -618,7 +634,7 @@
         ],
         input_output_aliases={0: 0},
         compiler_params=pltpu.CompilerParams(vmem_limit_bytes=GRANT),
-    )(up, own, *arrived, lows, turned, scales, late_scale)
+    )(up, near, own, *arrived, lows, turned, scales, late_scale)
     return gate.T, up.T, scale_gate, scale_up, norm
 
 

time: 777 us -> 775 us (level)
  transfers between devices with their start and end apart: 3 -> 2, of which waited for: 0 -> 0; matrix products, arithmetic and copies ran while one was open for 0% -> 0% of each run, Pallas kernels for 2% -> 2%
where the time goes in v4:
time: 775 us; the launch traced here: 774 us
  Pallas kernels  772 us (100%)
    pallas_call x1, Pallas kernels, exchange(): pl.pallas_call(functools.partial(exchange_kernel, n, groups), in_specs=[h...  758 us
  transfers between devices with their start and end apart: 2, of which 0 were waited for; matrix products, arithmetic and copies ran while one was open for 0% of the time, Pallas kernels for 2%

profile of v4, /device:TPU:0, one launch (start us, length us, event | category | flops | bytes accessed | tf_op | source)
XLA Modules:
  0.0 774.3 jit_solution(11979639773845474053)
XLA Ops:
  0.6 757.8 %shard_map.119 = (bf16[2,1728,5120]{2,1,0:T(8,128)(2,1)S(1)}, f32[2,1728,1]{2,1,0:T(8,128)S(1)}, f32[8,1,640]{2,1,0:T(1,128)S(1)}, bf16[2,4,32,1280]{3,2,1,0:T(8...) custom-call(bf16[1280,6912]{1,0:T(8,128)(2,1)} %weight_gate.1, ...), custom_call_target="tpu_custom_call" | custom-call | flops 1132462080 | bytes 70778880 | tf_op jit(solution)/shard_map/pallas_call | solution.py:550
  758.5 1.3 collective-permute-start
  759.8 0.4 collective-permute-start.1
  760.2 0.0 copy-start
  760.2 12.0 %shard_map.120 = (bf16[1728,5120]{1,0:T(8,128)(2,1)}, bf16[1728,5120]{1,0:T(8,128)(2,1)}, f32[1728]{0:T(1024)}, bf16[5120]{0:T(1024)(128)(2,1)}, f32[128,1]{1,0:T(8,128)S(1)}) custom-call(bf16[2,1728,5120]{2,1,0:T(8,128)(2,1)S(1)} %get-tuple-element.21.final, f32[2,1728,1]{2,1,0:T(8,128)S(1)} %get-tuple-element.22.scales, ...), custom_call_target="tpu_custom_call" | custom-call | flops 1132462080 | bytes 70778880 | tf_op jit(solution)/shard_map/pallas_call | solution.py:602
  772.2 0.0 collective-permute-done.from_2
  772.2 0.0 collective-permute-done.1.from_3
  772.2 0.0 copy-done
  772.2 2.1 shard_map.121
Async XLA Ops:
  758.5 13.8 %collective-permute-start = (bf16[64,1280]{1,0:T(8,128)(2,1)}, bf16[64,1280]{1,0:T(8,128)(2,1)S(1)}, u32[]{:S(2)}, u32[]{:S(2)}) collective-permute-start(bf16[64,1280]{1,0:T(8,128)(2,1)} %get-tuple-element.30), channel_id=1, source_target_pairs={{0,4},{2,6},{4,0},{6,2},{1,5},{3,7},{5,1},{7,3},{8,12},{10,14},{12... | collective-permute-start | bytes 491528 | tf_op jit(solution)/shard_map/ppermute | solution.py:595
  759.8 12.4 %collective-permute-start.1 = (bf16[64,1280]{1,0:T(8,128)(2,1)}, bf16[64,1280]{1,0:T(8,128)(2,1)S(1)}, u32[]{:S(2)}, u32[]{:S(2)}) collective-permute-start(bf16[64,1280]{1,0:T(8,128)(2,1)} %get-tuple-element.31), channel_id=1, source_target_pairs={{0,6},{2,4},{4,2},{6,0},{1,7},{3,5},{5,3},{7,1},{8,14},{10,12},{12... | collective-permute-start | bytes 491528 | tf_op jit(solution)/shard_map/ppermute | solution.py:596
  760.2 12.0 %copy-start = (bf16[64,1280]{1,0:T(8,128)(2,1)S(1)}, bf16[64,1280]{1,0:T(8,128)(2,1)}, u32[]{:S(2)}) copy-start(bf16[64,1280]{1,0:T(8,128)(2,1)} %get-tuple-element.29.own) | copy-start | bytes 491524
